TPU v7x, 256 devices: a whole 4x4x8 slice. The times are simulated.
256 devices in a mesh: cls: 8 (over x, y_hi), str: 32 (over z, y_lo, core).
Axes of the slice: x: 4, y: 4 (y_hi: 2, y_lo: 2; y = y_hi * 2 + y_lo), z: 8, core: 2. Of those that a mesh axis runs over, the one named last changes fastest.
Arguments:
- first_factor_tiles: float32 [8, 1024, 2, 4, 1024], P(None, ('cls', 'str')), may hold values from -6 to 6
- b_blocks: float32 [8, 1024, 2, 4, 512], P(None, ('cls', 'str')), may hold values from -0.0625 to 0.0625
Outputs:
- c_blocks: float32 [8, 1024, 2, 4, 512], P(None, ('cls', 'str'))
All inputs are finite; a program needn't handle non-finite values.
Results may differ from a plain program's by a relative error of at most 0.0003.
Values sent between devices are 32-bit elements; how exact they have to be, the bound alone decides.
A program may use at most 64 MiB of HBM per device.

v0:
```python
import math

import jax
import jax.numpy as jnp
from jax import lax
from jax.sharding import Mesh
from jax.sharding import PartitionSpec as P

CLS = ("cls_0", "cls_1")
CLS_STR = ("cls_0", "cls_1", "str")


def sent_together(arrays, axis, split_dim, concat_dim, along):
    widths = [math.prod(a.shape[along:]) for a in arrays]
    both = jnp.concatenate(
        [a.reshape(*a.shape[:along], w) for a, w in zip(arrays, widths)], axis=along
    )
    whole = lax.all_to_all(both, axis, split_axis=split_dim, concat_axis=concat_dim, tiled=True)
    tiles = jnp.split(whole, [sum(widths[:k]) for k in range(1, len(widths))], axis=along)
    return tuple((b.reshape(*whole.shape[:along], *a.shape[along:]) for a, b in zip(arrays, tiles)))


def summed_rows(subtotal, axes):
    for axis in axes:
        subtotal = lax.psum_scatter(subtotal, axis, scatter_dimension=0, tiled=True)
    return subtotal


def classical_tiles(first_factor_tiles, b_blocks, class_count, sub_count, per_device, highest):
    row_count = first_factor_tiles.shape[1]
    block_order = first_factor_tiles.shape[4]
    vertical_line_total = b_blocks.shape[4]
    group_cols = sub_count // 8
    col_width = 8 * vertical_line_total // group_cols
    a_rows = first_factor_tiles.reshape(8, row_count, class_count, per_device, block_order)
    send_inner_left = jnp.transpose(a_rows, (2, 0, 1, 3, 4))
    send_inner_right = b_blocks.reshape(class_count, per_device, row_count, 8 * vertical_line_total)
    got_left, got_right = sent_together((send_inner_left, send_inner_right), CLS, 0, 0, 1)
    tiled_left = jnp.repeat(jnp.transpose(got_left, (1, 0, 2, 3, 4)), group_cols, axis=0)
    split_right = got_right.reshape(class_count, per_device, row_count, group_cols, col_width)
    tiled_right = jnp.tile(jnp.transpose(split_right, (3, 0, 1, 2, 4)), (8, 1, 1, 1, 1))
    landed_left, landed_right = sent_together((tiled_left, tiled_right), "str", 0, 0, 2)
    left_block = jnp.transpose(landed_left, (1, 0, 2, 3, 4)).reshape(
        block_order, per_device * block_order
    )
    right_block = jnp.transpose(landed_right, (2, 1, 0, 3, 4)).reshape(
        per_device * block_order, col_width
    )
    own_part = summed_rows(
        jnp.dot(left_block, right_block, precision=highest, preferred_element_type=jnp.float32), CLS
    )
    returned = lax.all_to_all(
        own_part.reshape(sub_count, row_count, col_width),
        "str",
        split_axis=0,
        concat_axis=0,
        tiled=True,
    )
    arranged = jnp.transpose(returned.reshape(8, group_cols, row_count, col_width), (0, 2, 1, 3))
    return arranged.reshape(8, row_count, 2, 4, vertical_line_total)


def local(first_factor_tiles, b_blocks):
    highest = lax.Precision.HIGHEST
    class_count = lax.axis_size(CLS)
    sub_count = lax.axis_size("str")
    per_device = 8 // class_count
    return classical_tiles(
        first_factor_tiles, b_blocks, class_count, sub_count, per_device, highest
    )


def solution(mesh):
    split = Mesh(mesh.devices.reshape(4, 2, mesh.shape["str"]), ("cls_0", "cls_1", "str"))
    in_specs = (P(None, CLS_STR, None, None, None), P(None, CLS_STR, None, None, None))
    out_specs = P(None, CLS_STR, None, None, None)
    return jax.shard_map(local, mesh=split, in_specs=in_specs, out_specs=out_specs, check_vma=False)
```

profile of v0, /device:TPU:1, one launch (start us, length us, event | category | flops | bytes accessed | tf_op | source)
XLA Modules:
  0.0 392.3 jit_solution(8504334438173303490)
XLA Ops:
  6.5 0.0 reduce-scatter.3.cloned.1.call-start
  6.5 1.4 reshape_reshape.9
  7.9 1.6 reshape.37
  9.5 0.1 pad_maximum_fusion.1
  9.7 1.1 all_to_all.14
  10.8 28.3 %all_to_all.22 = f32[8,1,49152]{2,1,0:T(1,128)S(1)} all-to-all(f32[8,1,49152]{2,1,0:T(1,128)S(1)} %all_to_all.14), channel_id=1, replica_groups=mesh['cls_0'=4,'cls_1'=2,'str'=32] {'cls_0','cls_1'}, dimensions={0} | all-to-all | bytes 3145728 | tf_op jit(solution)/shard_map/all_to_all | solution.py:18
  39.1 0.9 copy.21
  40.0 0.1 split.16
  40.1 0.4 reshape_reshape.11
  40.5 0.3 copy.10
  40.8 0.5 broadcast_in_dim.3
  41.3 2.5 tile.11
  43.8 2.9 pad_maximum_fusion
  46.7 196.1 %all_to_all.23 = f32[32,8,8192]{2,1,0:T(8,128)S(1)} all-to-all(f32[32,8,8192]{2,1,0:T(8,128)S(1)} %pad_maximum_fusion), channel_id=1, replica_groups=mesh['cls_0'=4,'cls_1'=2,'str'=32] {'str'}, dimensions={0} | all-to-all | bytes 16777216 | tf_op jit(solution)/shard_map/all_to_all | solution.py:18
  242.8 2.7 fusion
  245.6 4.7 %copy.19 = f32[32,8,1,4,1024]{4,3,0,1,2:T(4,128)} copy(f32[32,8,1,4,1024]{4,1,3,0,2:T(8,128)S(1)} %bitcast.36) | data formatting | bytes 8388608 | tf_op jit(solution)/shard_map/reshape | solution.py:20
  250.2 5.3 %reshape.43 = f32[1024,1024]{1,0:T(8,128)} reshape(f32[1,8,32,4,1024]{4,3,2,1,0:T(4,128)} %bitcast.32) | data formatting | bytes 8388608 | tf_op jit(solution)/shard_map/reshape | solution.py:46
  255.5 6.8 %copy.20 = f32[32,8,4,1,1024]{4,2,0,1,3:T(4,128)} copy(f32[32,8,4,1,1024]{4,1,2,0,3:T(8,128)} %bitcast.35) | data formatting | bytes 8388608 | tf_op jit(solution)/shard_map/reshape | solution.py:20
  262.3 5.3 %reshape.41 = f32[1024,1024]{1,0:T(8,128)} reshape(f32[8,32,4,1,1024]{4,2,1,0,3:T(4,128)} %bitcast.33) | data formatting | bytes 8388608 | tf_op jit(solution)/shard_map/reshape | solution.py:43
  267.6 17.6 %fusion.1 = f32[1024,1024]{1,0:T(8,128)} fusion(f32[1024,1024]{1,0:T(8,128)} %reshape.41, f32[1024,1024]{1,0:T(8,128)} %reshape.43), kind=kOutput, calls=%fused_computation.7 | convolution fusion | flops 12884901888 | bytes 12582912 | tf_op jit(solution)/shard_map/dot_general | solution.py:50
  285.2 0.0 reduce-scatter.3.cloned.1.call-update
  285.2 0.0 reduce-scatter.5.cloned.1.call-start
  285.3 44.0 %reduce-scatter.3.cloned.1.call-done = f32[256,1024]{1,0:T(8,128)} async-done(((f32[1024,1024]{1,0:T(8,128)}), f32[256,1024]{1,0:T(8,128)}) %reduce-scatter.3.cloned.1.call-update) | async-done | bytes 1048592 | tf_op jit(solution)/shard_map/reduce_scatter | solution.py:25
  329.2 0.0 reduce-scatter.5.cloned.1.call-update
  329.3 29.2 %reduce-scatter.5.cloned.1.call-done = f32[128,1024]{1,0:T(8,128)} async-done(((f32[256,1024]{1,0:T(8,128)}), f32[128,1024]{1,0:T(8,128)}) %reduce-scatter.5.cloned.1.call-update) | async-done | bytes 524304 | tf_op jit(solution)/shard_map/reduce_scatter | solution.py:25
  358.4 1.2 reshape.44
  359.6 24.4 %all_to_all.24 = f32[32,4,1024]{2,1,0:T(4,128)S(1)} all-to-all(f32[32,4,1024]{2,1,0:T(4,128)S(1)} %reshape.44), channel_id=1, replica_groups=mesh['cls_0'=4,'cls_1'=2,'str'=32] {'str'}, dimensions={0} | all-to-all | bytes 1048576 | tf_op jit(solution)/shard_map/all_to_all | solution.py:52
  384.0 0.3 copy.22
  384.3 1.2 reshape.46
  (1 shorter events, 0.0 us)
Async XLA Ops:
  6.5 322.7 %reduce-scatter.3.cloned.1.call-start = ((), (), s32[]{:S(2)}) async-start(), calls=%async_computation.5 | async-start | bytes 5242880 | tf_op jit(solution)/shard_map/reduce_scatter | solution.py:25
  285.2 73.2 %reduce-scatter.5.cloned.1.call-start = ((), (), s32[]{:S(2)}) async-start(), calls=%async_computation.6 | async-start | bytes 1572864 | tf_op jit(solution)/shard_map/reduce_scatter | solution.py:25
Sparse Core Ops, SparseCore 0:
  285.3 43.8 reduce-scatter.2
  331.7 26.6 reduce-scatter.4
where the time goes:
time: 393 us; the launch traced here: 392 us
  blocking collectives  249 us (63%)
  waiting for transfers between devices  73.2 us (19%)
  local copies, waits for them, and re-layouts  36.3 us (9%)
  matrix products  17.6 us (4%)
  between operations  13.5 us (3%)
    all_to_all x2, blocking collectives, sent_together(): lax.all_to_all(both, axis, split_axis=split_dim, concat_axis=concat_dim,...  224 us
    reduce_scatter x2, waiting for transfers between devices, summed_rows(): subtotal = lax.psum_scatter(subtotal, axis, scatter_dimension=0, tiled=True)  73.2 us
    all_to_all x1, blocking collectives, classical_tiles(): lax.all_to_all(own_part.reshape(sub_count, row_count, col_width), 'str',...  24.4 us
    dot_general x1, matrix products, classical_tiles(): jnp.dot(left_block, right_block, precision=highest, preferred_element_typ...  17.6 us
    reshape x2, local copies, waits for them, and re-layouts, sent_together(): b.reshape(*whole.shape[:along], *a.shape[along:])  11.5 us
  transfers between devices with their start and end apart: 2, of which 2 were waited for; matrix products, arithmetic and copies ran while one was open for 0% of the time, Pallas kernels for 0%

commit v1 on v0

v1 whole, which is shorter than its diff:
```python
import functools

import jax
import jax.numpy as jnp
from jax import lax
from jax.experimental import pallas as pl
from jax.experimental.pallas import tpu as pltpu
from jax.sharding import PartitionSpec as P

MESH = pl.DeviceIdType.MESH
COLUMN_PARTS = 2


class Plan:
    def __init__(self, nx, ny, nz, nc):
        self.nx, self.ny, self.nz, self.nc = nx, ny, nz, nc
        self.yl = min(2, ny)
        self.yh = ny // self.yl
        self.nyc = ny * nc

    def here(self):
        cls, sub = lax.axis_index("cls"), lax.axis_index("str")
        core = lax.rem(sub, self.nc)
        low = lax.rem(sub // self.nc, self.yl)
        z = sub // (self.nc * self.yl)
        x, high = cls // self.yh, lax.rem(cls, self.yh)
        return x, high * self.yl + low, z, core

    def device(self, x, y, z, core):
        return (
            x * self.yh + y // self.yl,
            (z * self.yl + lax.rem(y, self.yl)) * self.nc + core,
        )


def split_bf16(value):
    high = value.astype(jnp.bfloat16)
    low = (value - high.astype(jnp.float32)).astype(jnp.bfloat16)
    return high, low


def kernel(plan, a_ref, b_ref, c_ref, at, bt, ah, al, bh, bl, part, turn, got, total, back, send, recv):
    nx, ny, nz, nc, nyc = plan.nx, plan.ny, plan.nz, plan.nc, plan.nyc
    x, y, z, core = plan.here()
    yc = y * nc + core
    count = [0]

    def xmod(k):
        return lax.rem(x + (k + 4 * nx), nx)

    def ymod(k):
        return lax.rem(y + (k + 4 * ny), ny)

    def zmod(k):
        return lax.rem(z + (k + 4 * nz), nz)

    def ycmod(k):
        return lax.rem(yc + (k + 4 * nyc), nyc)

    def yc_device(k):
        other = ycmod(k)
        return plan.device(x, other // nc, z, lax.rem(other, nc))

    started = []

    def push(src, dst, device):
        k = count[0]
        count[0] += 1
        copy = pltpu.make_async_remote_copy(
            src_ref=src,
            dst_ref=dst,
            send_sem=send.at[k],
            recv_sem=recv.at[k],
            device_id=device,
            device_id_type=MESH,
        )
        copy.start()
        started.append(copy)
        return copy

    barrier = pltpu.get_barrier_semaphore()
    friends = [plan.device(xmod(k), y, z, core) for k in range(1, nx)]
    friends += [yc_device(k) for k in range(1, nyc)]
    if nz > 1:
        friends += [plan.device(x, y, zmod(1), core), plan.device(x, y, zmod(-1), core)]
    for friend in friends:
        pl.semaphore_signal(barrier, inc=1, device_id=friend, device_id_type=MESH)
    pl.semaphore_wait(barrier, len(friends))

    x_next, x_prev = plan.device(xmod(1), y, z, core), plan.device(xmod(-1), y, z, core)
    y_next, y_prev = plan.device(x, ymod(1), z, core), plan.device(x, ymod(-1), z, core)
    z_next, z_prev = plan.device(x, y, zmod(1), core), plan.device(x, y, zmod(-1), core)

    b_in = [push(b_ref.at[ycmod(k)], bt.at[z, yc], yc_device(k)) for k in range(1, nyc)]
    order = [k for k in (1, 3, 2) if k < nx]
    a_in = {k: push(a_ref.at[xmod(k)], at.at[x, yc], plan.device(xmod(k), y, z, core)) for k in order}
    bt[z, yc] = b_ref[yc]

    def a_source(k, ys):
        if k == 0 and ys == 0:
            return a_ref.at[x]
        return at.at[xmod(-k), ymod(ys) * nc + core]

    near, far, pair = {}, {}, {}

    def spread(k):
        src = a_source(k, 0)
        dst = at.at[xmod(-k), yc]
        if ny > 1:
            near[k, -1] = push(src, dst, y_next)
            near[k, 1] = push(src, dst, y_prev)
        give_partner(k, 0)

    def give_partner(k, ys):
        if nc > 1:
            there = plan.device(x, y, z, 1 - core)
            pair[k, ys] = push(a_source(k, ys), at.at[xmod(-k), ymod(ys) * nc + core], there)

    def cut_a(k, ys, own):
        other = core if own else 1 - core
        slot = ymod(ys) * nc + other
        xs = xmod(-k)
        rows = pl.ds(pl.multiple_of(slot * 32, 32), 32)
        value = a_ref[x] if own and k == 0 and ys == 0 else at[xs, slot]
        high, low = split_bf16(value)
        ah[xs, rows, :] = high
        al[xs, rows, :] = low

    depth = a_ref.shape[2] // 8
    group = plan.yl * nc

    def cut_b(zs, half):
        def one(b, _):
            rows = bt[zs, pl.ds(half * group, group), b].reshape(group * 4, bt.shape[4])
            high, low = split_bf16(rows)
            first = b * depth + half * (depth // plan.yh) + zs * (group * 4)
            where = pl.ds(pl.multiple_of(first, group * 4), group * 4)
            bh[where, :] = high
            bl[where, :] = low
            return 0

        lax.fori_loop(0, 8, one, 0)

    rings = {}

    def ring(direction, half, hop):
        held = zmod(-direction * (hop - 1))
        there = bt.at[held, pl.ds(half * group, group)]
        rings[direction, half, hop] = push(there, there, z_next if direction == 1 else z_prev)

    def last_hop(direction, half):
        long = (half == 0) == (direction == 1)
        return nz // 2 if long else (nz - 1) // 2

    halves = range(plan.yh)
    if plan.yh == 1:
        def last_hop(direction, half):
            return nz // 2 if direction == 1 else (nz - 1) // 2

    events = []

    def at_time(when, act):
        events.append((when, len(events), act))

    def b_arrived():
        for copy in b_in:
            copy.wait_recv()
        if nz > 1:
            for half in halves:
                for direction in (1, -1):
                    ring(direction, half, 1)
        for half in halves:
            cut_b(z, half)

    def ring_arrived(direction, half, hop):
        rings[direction, half, hop].wait_recv()
        if hop < last_hop(direction, half):
            ring(direction, half, hop + 1)
        cut_b(zmod(-direction * hop), half)

    def x_arrived(k):
        a_in[k].wait_recv()
        spread(k)
        cut_a(k, 0, True)

    def near_arrived(k, ys):
        near[k, ys].wait_recv()
        if ny == 4 and (ys == -1) == (k in (0, 3)):
            src = a_source(k, ys)
            far[k] = push(src, src, y_next if ys == -1 else y_prev)
        give_partner(k, ys)
        cut_a(k, ys, True)

    def far_arrived(k):
        far[k].wait_recv()
        give_partner(k, 2)
        cut_a(k, 2, True)

    def pair_arrived(k, ys):
        pair[k, ys].wait_recv()
        cut_a(k, ys, False)

    spread(0)
    cut_a(0, 0, True)
    at_time(5.0, b_arrived)
    ready = {0: 3.0, 1: 9.0, 3: 9.2, 2: 15.0}
    sent_at = {0: 10.0, 1: 17.0, 3: 23.0, 2: 34.0}
    far_at = {0: 29.0, 1: 29.2, 3: 40.0, 2: 41.0}
    for k in [0, *order]:
        if k:
            at_time(ready[k], functools.partial(x_arrived, k))
        if nc > 1:
            at_time(ready[k] + 3.0, functools.partial(pair_arrived, k, 0))
        if ny > 1:
            for ys in (-1, 1):
                at_time(sent_at[k], functools.partial(near_arrived, k, ys))
                if nc > 1:
                    at_time(sent_at[k] + 3.0, functools.partial(pair_arrived, k, ys))
        if ny == 4:
            at_time(far_at[k], functools.partial(far_arrived, k))
            if nc > 1:
                at_time(far_at[k] + 3.0, functools.partial(pair_arrived, k, 2))
    if nz > 1:
        for half in halves:
            for direction in (1, -1):
                for hop in range(1, last_hop(direction, half) + 1):
                    first = half if direction == 1 else 1 - half
                    at_time(7.0 + 5.5 * first + 11.0 * hop - 5.0, functools.partial(ring_arrived, direction, half, hop))
    for _, _, act in sorted(events, key=lambda e: e[:2]):
        act()

    width = bh.shape[1] // COLUMN_PARTS
    mid = nyc // 2
    lower, upper = pl.ds(0, mid), pl.ds(mid, nyc - mid)

    def product(n, k):
        xs = xmod(k)
        cols = pl.ds(n * width, width)
        right_high, right_low = bh[:, cols], bl[:, cols]
        left_high = ah[xs]
        value = jnp.dot(left_high, right_high, preferred_element_type=jnp.float32)
        value += jnp.dot(left_high, right_low, preferred_element_type=jnp.float32)
        value += jnp.dot(al[xs], right_high, preferred_element_type=jnp.float32)
        part[n, k] = value.reshape(nyc, 32, width)

    steps = {}
    for n in range(COLUMN_PARTS):
        if nx == 4:
            product(n, 2)
            steps[n, "turn", 0] = push(part.at[n, 2, lower], turn.at[n, 0], x_next)
            steps[n, "turn", 1] = push(part.at[n, 2, upper], turn.at[n, 1], x_prev)
            product(n, 1)
            steps[n, "got", 0, 1] = push(part.at[n, 1, upper], got.at[n, 0, upper], x_next)
            product(n, 3)
            steps[n, "got", 1, 0] = push(part.at[n, 3, lower], got.at[n, 1, lower], x_prev)
        product(n, 0)

    def pass_on(n):
        if nx == 4:
            steps[n, "turn", 0].wait_recv()
            part[n, 1, lower] += turn[n, 0]
            steps[n, "turn", 1].wait_recv()
            part[n, 3, upper] += turn[n, 1]
            steps[n, "got", 0, 0] = push(part.at[n, 1, lower], got.at[n, 0, lower], x_next)
            steps[n, "got", 1, 1] = push(part.at[n, 3, upper], got.at[n, 1, upper], x_prev)

    def finish(n):
        value = part[n, 0]
        if nx == 4:
            for side in (0, 1):
                for half in (0, 1):
                    steps[n, "got", side, half].wait_recv()
            value = value + got[n, 0] + got[n, 1]
        total[n] = value
        back[yc, n] = total[n, yc]
        steps[n, "back"] = [push(total.at[n, ycmod(k)], back.at[yc, n], yc_device(k)) for k in range(1, nyc)]

    for n in range(COLUMN_PARTS):
        pass_on(n)
    for n in range(COLUMN_PARTS):
        finish(n)
    for n in range(COLUMN_PARTS):
        for copy in steps[n, "back"]:
            copy.wait_recv()
    c_ref[...] = back[...]
    for copy in started:
        copy.wait_send()


def exchange_product(plan, a_parts, b_parts):
    nx, nz, nyc = plan.nx, plan.nz, plan.nyc
    inner, wide = a_parts.shape[2], b_parts.shape[3]
    width = wide // COLUMN_PARTS
    f32, bf16 = jnp.float32, jnp.bfloat16
    return pl.pallas_call(
        functools.partial(kernel, plan),
        out_shape=jax.ShapeDtypeStruct((nyc, COLUMN_PARTS, 32, width), f32),
        in_specs=[pl.BlockSpec(memory_space=pltpu.VMEM)] * 2,
        out_specs=pl.BlockSpec(memory_space=pltpu.VMEM),
        scratch_shapes=[
            pltpu.VMEM((nx, nyc, 32, inner), f32),
            pltpu.VMEM((nz, nyc, 8, 4, wide), f32),
            pltpu.VMEM((nx, nyc * 32, inner), bf16),
            pltpu.VMEM((nx, nyc * 32, inner), bf16),
            pltpu.VMEM((inner, wide), bf16),
            pltpu.VMEM((inner, wide), bf16),
            pltpu.VMEM((COLUMN_PARTS, nx, nyc, 32, width), f32),
            pltpu.VMEM((COLUMN_PARTS, 2, nyc // 2, 32, width), f32),
            pltpu.VMEM((COLUMN_PARTS, 2, nyc, 32, width), f32),
            pltpu.VMEM((COLUMN_PARTS, nyc, 32, width), f32),
            pltpu.VMEM((nyc, COLUMN_PARTS, 32, width), f32),
            pltpu.SemaphoreType.DMA((128,)),
            pltpu.SemaphoreType.DMA((128,)),
        ],
        compiler_params=pltpu.CompilerParams(
            collective_id=0, has_side_effects=True, vmem_limit_bytes=60 * 1024 * 1024
        ),
    )(a_parts, b_parts)


def local(plan, first_factor_tiles, b_blocks):
    b, i, h, c, r = first_factor_tiles.shape
    a_parts = first_factor_tiles.reshape(b * i, h * c, plan.nx, r // plan.nx)
    a_parts = jnp.transpose(a_parts, (2, 0, 1, 3)).reshape(plan.nx, b * i, h * c * r // plan.nx)
    wide = b_blocks.shape[4]
    b_parts = jnp.transpose(b_blocks.reshape(b, i, h * c, wide), (2, 0, 1, 3))
    out = exchange_product(plan, a_parts, b_parts)
    out = out.reshape(h, c, COLUMN_PARTS, b, i, wide // COLUMN_PARTS)
    return jnp.transpose(out, (3, 4, 0, 1, 2, 5)).reshape(b, i, h, c, wide)


def solution(mesh):
    plan = Plan(4, 4, mesh.shape["str"] // 4, 2)
    spec = P(None, ("cls", "str"), None, None, None)
    return jax.shard_map(
        functools.partial(local, plan), mesh=mesh, in_specs=(spec, spec), out_specs=spec, check_vma=False
    )
```

time: 393 us -> 98.3 us (0.25)
  blocking collectives: 249 us -> 0 us
  Pallas kernels: 0 us -> 90.7 us
  waiting for transfers between devices: 73.2 us -> 0 us
  local copies, waits for them, and re-layouts: 36.3 us -> 7.33 us
  matrix products: 17.6 us -> 0 us
  between operations: 13.5 us -> 0.04 us
    all_to_all x3 -> x0, blocking collectives: 249 us -> none  [the longest x2 224 us: sent_together(): lax.all_to_all(both, axis, split_axis=split_dim, concat_axis=concat_dim,...]
    pallas_call x0 -> x1, Pallas kernels: none -> 90.7 us  [exchange_product(): pl.pallas_call(functools.partial(kernel, plan), out_shape=jax.ShapeDtypeS...]
    reduce_scatter x2 -> x0, waiting for transfers between devices: 73.2 us -> none  [summed_rows(): subtotal = lax.psum_scatter(subtotal, axis, scatter_dimension=0, tiled=True)]
    reshape x8 -> x5, local copies, waits for them, and re-layouts: 26.3 us -> 5.79 us  [the longest x2 2.15 us: local(): a_parts = first_factor_tiles.reshape(b * i, h * c, plan.nx, r // plan.nx)]
    dot_general x1 -> x0, matrix products: 17.6 us -> none  [classical_tiles(): jnp.dot(left_block, right_block, precision=highest, preferred_element_typ...]
    another operation x4 -> x0, local copies, waits for them, and re-layouts: 4.57 us -> none  [the longest x2 2.8 us: classical_tiles(): jnp.tile(jnp.transpose(split_right, (3, 0, 1, 2, 4)), (8, 1, 1, 1, 1))]
  transfers between devices with their start and end apart: 2 -> 0, of which waited for: 2 -> 0; matrix products, arithmetic and copies ran while one was open for 0% -> 0% of each run, Pallas kernels for 0% -> 0%
where the time goes in v1:
time: 98.3 us; the launch traced here: 98.1 us
  Pallas kernels  90.7 us (92%)
  local copies, waits for them, and re-layouts  7.33 us (7%)
    pallas_call x1, Pallas kernels, exchange_product(): pl.pallas_call(functools.partial(kernel, plan), out_shape=jax.ShapeDtypeS...  90.7 us
    reshape x2, local copies, waits for them, and re-layouts, local(): a_parts = first_factor_tiles.reshape(b * i, h * c, plan.nx, r // plan.nx)  2.15 us

profile of v1, /device:TPU:1, one launch (start us, length us, event | category | flops | bytes accessed | tf_op | source)
XLA Modules:
  0.0 98.1 jit_solution(15735295809549987767)
XLA Ops:
  0.0 1.9 %reshape.15 = f32[32,8,4,256]{3,2,1,0:T(4,128)S(1)} reshape(f32[8,4,2,4,1024]{4,3,2,1,0:T(4,128)} %param.2) | data formatting | bytes 2097152 | tf_op jit(solution)/shard_map/reshape | solution.py:323
  1.9 0.2 copy.7
  2.2 0.0 copy-start
  2.2 1.1 %reshape.16.a_ref = f32[4,32,2048]{2,1,0:T(8,128)} reshape(f32[4,32,8,256]{3,2,1,0:T(8,128)S(1)} %bitcast.11) | data formatting | bytes 2097152 | tf_op jit(solution)/shard_map/reshape | solution.py:324
  3.3 0.0 copy-done
  3.3 1.1 %copy.4 = f32[8,4,2,4,512]{4,1,0,3,2:T(4,128)} copy(f32[8,4,2,4,512]{4,3,2,1,0:T(4,128)S(1)} %copy-done) | data formatting | bytes 1048576 | tf_op args[1]
  4.5 90.7 %shard_map.28 = f32[8,2,32,256]{3,2,1,0:T(8,128)} custom-call(f32[4,32,2048]{2,1,0:T(8,128)} %reshape.16.a_ref, f32[8,8,4,512]{3,2,1,0:T(4,128)} %bitcast.13), custom_call_target="tpu_custom_call" | custom-call | tf_op jit(solution)/shard_map/pallas_call | solution.py:295
  95.2 1.2 %reshape.18 = f32[2,4,2,8,4,256]{5,4,3,2,1,0:T(4,128)S(1)} reshape(f32[8,2,32,256]{3,2,1,0:T(8,128)} %shard_map.28) | data formatting | bytes 1048576 | tf_op jit(solution)/shard_map/reshape | solution.py:328
  96.4 0.4 copy.5
  96.8 1.3 %reshape.19 = f32[8,4,2,4,512]{4,3,2,1,0:T(4,128)} reshape(f32[8,4,2,4,2,256]{5,4,3,2,1,0:T(2,128)S(1)} %copy.5) | data formatting | bytes 1048576 | tf_op jit(solution)/shard_map/reshape | solution.py:329
Async XLA Ops:
  2.2 1.2 %copy-start = (f32[8,4,2,4,512]{4,3,2,1,0:T(4,128)S(1)}, f32[8,4,2,4,512]{4,3,2,1,0:T(4,128)}, u32[]{:S(2)}) copy-start(f32[8,4,2,4,512]{4,3,2,1,0:T(4,128)} %param.3) | copy-start | bytes 1572868

commit v2 on v1

v2 whole, which is shorter than its diff:
```python
import functools

import jax
import jax.numpy as jnp
from jax import lax
from jax.experimental import pallas as pl
from jax.experimental.pallas import tpu as pltpu
from jax.sharding import PartitionSpec as P

MESH = pl.DeviceIdType.MESH
WIDTHS = (384, 128)
LAG, CUT_A, CUT_B, DOT = 2.8, 0.2, 0.25, 0.0022
GROUPS = {
    (0, 0): ((2,), (1,), (3,), (0,)),
    (0, 1): ((2, 1), (3, 0)),
    (1, 0): ((2, 1, 3, 0),),
    (1, 1): ((2, 1, 3, 0),),
}
HOLD = (3, 2)


class Plan:
    def __init__(self, nx, ny, nz, nc):
        self.nx, self.ny, self.nz, self.nc = nx, ny, nz, nc
        self.yl = min(2, ny)
        self.yh = ny // self.yl
        self.nyc = ny * nc

    def here(self):
        cls, sub = lax.axis_index("cls"), lax.axis_index("str")
        core = lax.rem(sub, self.nc)
        low = lax.rem(sub // self.nc, self.yl)
        z = sub // (self.nc * self.yl)
        x, high = cls // self.yh, lax.rem(cls, self.yh)
        return x, high * self.yl + low, z, core

    def device(self, x, y, z, core):
        return (
            x * self.yh + y // self.yl,
            (z * self.yl + lax.rem(y, self.yl)) * self.nc + core,
        )


def split_bf16(value):
    high = value.astype(jnp.bfloat16)
    low = (value - high.astype(jnp.float32)).astype(jnp.bfloat16)
    return high, low


def kernel(plan, a_hbm, b_hbm, c_ref, asrc, at, ah, al, bsrc, bt, bhl, part, turn, got, total, back, a_in_ref, b_in_ref, load, send, recv):
    nx, ny, nz, nc, nyc = plan.nx, plan.ny, plan.nz, plan.nc, plan.nyc
    x, y, z, core = plan.here()
    yc = y * nc + core
    chunks = range(len(bt))
    widths = [ref.shape[4] for ref in bt]
    count = [0]
    started = []

    def xmod(k):
        return lax.rem(x + (k + 4 * nx), nx)

    def ymod(k):
        return lax.rem(y + (k + 4 * ny), ny)

    def zmod(k):
        return lax.rem(z + (k + 4 * nz), nz)

    def cmod(k):
        return lax.rem(core + k, nc)

    def push(src, dst, device):
        k = count[0]
        count[0] += 1
        copy = pltpu.make_async_remote_copy(
            src_ref=src,
            dst_ref=dst,
            send_sem=send.at[k],
            recv_sem=recv.at[k],
            device_id=device,
            device_id_type=MESH,
        )
        copy.start()
        started.append(copy)
        return copy

    b_load = pltpu.make_async_copy(b_hbm, b_in_ref, load.at[0])
    a_load = pltpu.make_async_copy(a_hbm, a_in_ref, load.at[1])
    b_load.start()
    a_load.start()
    barrier = pltpu.get_barrier_semaphore()
    near_first = [k for k in (1, 3, 2) if k < ny]
    others = [(k, q) for k in [0, *near_first] for q in range(nc) if k or q]
    friends = [plan.device(xmod(k), y, z, core) for k in range(1, nx)]
    friends += [plan.device(x, ymod(k), z, cmod(q)) for k, q in others]
    if nz > 1:
        friends += [plan.device(x, y, zmod(1), core), plan.device(x, y, zmod(-1), core)]
    for friend in friends:
        pl.semaphore_signal(barrier, inc=1, device_id=friend, device_id_type=MESH)

    a_ref, b_ref = a_in_ref, b_in_ref
    b_load.wait()

    nb, ni, nh, _, deep = a_ref.shape
    per_x = deep // nx
    for slot in range(nyc):
        h, c = divmod(slot, b_ref.shape[3])
        first = 0
        for n in chunks:
            bsrc[n][slot] = b_ref[:, :, h, c, first : first + widths[n]]
            first += widths[n]
    for n in chunks:
        bt[n][z, yc] = bsrc[n][yc]
    a_load.wait()
    for k in range(nx):
        for hc in range(nb):
            h, c = divmod(hc, nb // nh)
            rows = a_ref[:, :, h, c, k * per_x : (k + 1) * per_x].reshape(nb * ni, per_x)
            asrc[k, :, hc * per_x : (hc + 1) * per_x] = rows

    pl.semaphore_wait(barrier, len(friends))

    x_next, x_prev = plan.device(xmod(1), y, z, core), plan.device(xmod(-1), y, z, core)
    y_next, y_prev = plan.device(x, ymod(1), z, core), plan.device(x, ymod(-1), z, core)
    z_next, z_prev = plan.device(x, y, zmod(1), core), plan.device(x, y, zmod(-1), core)

    b_in = {}

    def send_b(n):
        for k, q in others:
            there = ymod(k) * nc + cmod(q)
            b_in[n, k, q] = push(bsrc[n].at[there], bt[n].at[z, yc], plan.device(x, ymod(k), z, cmod(q)))

    send_b(0)
    order = [k for k in (1, 3, 2) if k < nx]
    a_in = {k: push(asrc.at[xmod(k)], at.at[x, yc], plan.device(xmod(k), y, z, core)) for k in order}

    def a_source(k, ys):
        if k == 0 and ys == 0:
            return asrc.at[x]
        return at.at[xmod(-k), ymod(ys) * nc + core]

    near, far, pair = {}, {}, {}

    def spread(k):
        src = a_source(k, 0)
        dst = at.at[xmod(-k), yc]
        if ny > 1:
            near[k, 3] = push(src, dst, y_next)
            near[k, 1] = push(src, dst, y_prev)
        give_partner(k, 0)

    def give_partner(k, ys):
        if nc > 1:
            there = plan.device(x, y, z, cmod(1))
            pair[k, ys] = push(a_source(k, ys), at.at[xmod(-k), ymod(ys) * nc + core], there)

    row_parts = [[k for k in (0, 1, 3) if k < ny], [k for k in (2,) if k < ny]]
    place = {k: (j, p) for j, ks in enumerate(row_parts) for p, k in enumerate(ks)}

    def cut_a(k, ys, own):
        other = core if own else cmod(1)
        j, p = place[ys]
        where = pl.ds(pl.multiple_of((p * nc + other) * 32, 32), 32)
        value = asrc[x] if own and k == 0 and ys == 0 else at[xmod(-k), ymod(ys) * nc + other]
        high, low = split_bf16(value)
        ah[j][k, where, :] = high
        al[j][k, where, :] = low

    depth = asrc.shape[2] // nb
    group = plan.yl * nc

    def cut_b(n, zs):
        def one(b, _):
            for half in range(plan.yh):
                rows = bt[n][zs, pl.ds(half * group, group), b].reshape(group * 4, widths[n])
                high, low = split_bf16(rows)
                first = b * depth + half * (depth // plan.yh) + zs * (group * 4)
                where = pl.ds(pl.multiple_of(first, group * 4), group * 4)
                bhl[n][where, : widths[n]] = high
                bhl[n][where, widths[n] :] = low
            return 0

        lax.fori_loop(0, nb, one, 0)

    groups = {0: [(ymod(k) * nc, nc, k in (0, 1)) for k in [0, *near_first]]}
    wide = max(1, nyc // 2) if ny > 1 else nyc
    for n in chunks[1:]:
        groups[n] = [(first, wide, first == 0) for first in range(0, nyc, wide)]
    rings = {}

    def last_hop(n, g, up):
        return nz // 2 if groups[n][g][2] == up else (nz - 1) // 2

    def ring(n, g, up, hop):
        first, slots, _ = groups[n][g]
        there = bt[n].at[zmod(1 - hop if up else hop - 1), pl.ds(first, slots)]
        rings[n, g, up, hop] = push(there, there, z_next if up else z_prev)

    def b_arrived(n, g):
        keys = list(others)
        if n == 0:
            far_y = [0, *near_first][g]
            keys = [(k, q) for k, q in others if (k + far_y) % ny == 0]
        elif g:
            keys = []
        for k, q in keys:
            b_in[n, k, q].wait_recv()
        for up in (True, False):
            if last_hop(n, g, up):
                ring(n, g, up, 1)
        if g == len(groups[n]) - 1:
            cut_b(n, z)

    def ring_arrived(n, g, hop):
        for up in (True, False):
            if hop <= last_hop(n, g, up):
                rings[n, g, up, hop].wait_recv()
                if hop < last_hop(n, g, up):
                    ring(n, g, up, hop + 1)
        if g == len(groups[n]) - 1:
            cut_b(n, zmod(hop))
            if 2 * hop != nz:
                cut_b(n, zmod(-hop))

    def x_arrived(k):
        a_in[k].wait_recv()
        spread(k)
        cut_a(k, 0, True)

    def near_arrived(k, ys):
        near[k, ys].wait_recv()
        give_partner(k, ys)
        cut_a(k, ys, True)

    def pass_far(k):
        ys = 3 if k in (0, 3) else 1
        src = a_source(k, ys)
        far[k] = push(src, src, y_next if ys == 3 else y_prev)

    def far_arrived(k):
        far[k].wait_recv()
        give_partner(k, 2)
        cut_a(k, 2, True)

    def pair_arrived(k, ys):
        pair[k, ys].wait_recv()
        cut_a(k, ys, False)

    steps = {}

    def halves(j):
        slots = len(row_parts[j]) * nc
        return pl.ds(0, slots // 2), pl.ds(slots // 2, slots - slots // 2)

    def product(j, n, ds):
        width = widths[n]
        first = min((nx - d) % nx for d in ds)
        slots = len(row_parts[j]) * nc
        left_high = ah[j][first : first + len(ds)].reshape(len(ds) * slots * 32, ah[j].shape[2])
        left_low = al[j][first : first + len(ds)].reshape(len(ds) * slots * 32, ah[j].shape[2])
        both = jnp.dot(left_high, bhl[n][...], preferred_element_type=jnp.float32)
        value = jnp.dot(left_low, bhl[n][:, :width], preferred_element_type=jnp.float32)
        value = value + both[:, :width] + both[:, width:]
        value = value.reshape(len(ds), slots, 32, width)
        for d in ds:
            part[j][n][d] = value[(nx - d) % nx - first]
        for d in ds:
            send_part(j, n, d)

    def send_part(j, n, d):
        out = part[j][n]
        lower, upper = halves(j)
        if d == 2:
            steps[j, n, "turn", 0] = push(out.at[2, lower], turn[j][n].at[0, lower], x_next)
            steps[j, n, "turn", 1] = push(out.at[2, upper], turn[j][n].at[0, upper], x_prev)
        elif d == 1:
            steps[j, n, "got", 0, 1] = push(out.at[1, upper], got[j][n].at[0, upper], x_next)
        elif d == 3:
            steps[j, n, "got", 1, 0] = push(out.at[3, lower], got[j][n].at[1, lower], x_prev)

    def pass_on(j, n):
        if nx == 4:
            lower, upper = halves(j)
            out = part[j][n]
            steps[j, n, "turn", 0].wait_recv()
            out[1, lower] += turn[j][n][0, lower]
            steps[j, n, "turn", 1].wait_recv()
            out[3, upper] += turn[j][n][0, upper]
            steps[j, n, "got", 0, 0] = push(out.at[1, lower], got[j][n].at[0, lower], x_next)
            steps[j, n, "got", 1, 1] = push(out.at[3, upper], got[j][n].at[1, upper], x_prev)

    def finish(j, n):
        value = part[j][n][0]
        if nx == 4:
            for side in (0, 1):
                for half in (0, 1):
                    steps[j, n, "got", side, half].wait_recv()
            value = value + got[j][n][0] + got[j][n][1]
        total[j][n][...] = value
        for p, k in enumerate(row_parts[j]):
            for q in range(nc):
                src = total[j][n].at[p * nc + cmod(q)]
                if k or q:
                    there = plan.device(x, ymod(k), z, cmod(q))
                    steps[n, "back", k, q] = push(src, back[n].at[yc], there)
                else:
                    back[n][yc] = total[j][n][core]

    def hand_over(n):
        for k, q in others:
            steps[n, "back", k, q].wait_recv()
        first = sum(widths[:n])
        for slot in range(nyc):
            h, c = divmod(slot, c_ref.shape[3])
            c_ref[:, :, h, c, first : first + widths[n]] = back[n][slot].reshape(nb, ni, widths[n])

    acts = dict(
        send_b=send_b, b_arrived=b_arrived, ring_arrived=ring_arrived, x_arrived=x_arrived,
        near_arrived=near_arrived, pass_far=pass_far, far_arrived=far_arrived, pair_arrived=pair_arrived,
        product=product, pass_on=pass_on, finish=finish, hand_over=hand_over,
    )
    spread(0)
    cut_a(0, 0, True)
    inner = asrc.shape[2]
    plans = schedule(plan, order, near_first, groups, last_hop, row_parts, chunks, widths, inner)
    for _, act, what in plans:
        acts[act](*what)
    for copy in started:
        copy.wait_send()


def schedule(plan, order, near_first, groups, last_hop, row_parts, chunks, widths, inner):
    steps, known, free, clock = [], {"go": 0.0}, {}, [0.0]
    rate = 46.0
    piece = 32 * inner * 4 / 1024.0

    def add(act, what, deps, sends=(), cost=0.0, rank=1):
        steps.append((act, what, deps, sends, cost, rank))

    def slot(n):
        return 32 * widths[n] * 4 / 1024.0

    def b_sends(n):
        return [(("b_in", n, k, q), {0: "d", 1: "yu", 2: ("yu", "yd")[q], 3: "yd"}[k], slot(n) * (2 if k == 2 else 1)) for k in [0, *near_first] for q in range(plan.nc) if k or q]

    add("send_b", (0,), ["go"], b_sends(0), 0.0, 0)
    add("x_send", (), [("send_b", 0)], [(("x", k), {1: "xu", 2: "xu", 3: "xd"}[k], piece) for k in order], 0.0, 0)
    for n in chunks[1:]:
        add("send_b", (n,), [("x_send",), ("spread", 0)], b_sends(n), 0.0, 0)

    def spread(k):
        sends = [(("near", k, 3), "yu", piece), (("near", k, 1), "yd", piece)] if near_first else []
        return sends + ([(("pair", k, 0), "d", piece)] if plan.nc > 1 else [])

    add("spread", (0,), [("x_send",)], spread(0), CUT_A, 0)
    for k in order:
        add("x_arrived", (k,), [("x", k)], spread(k), CUT_A, 0)
    all_x = [("x_arrived", k) for k in order]
    cuts = {j: [] for j in range(2)}
    cuts[0] += [("spread", 0), *all_x]
    for k in [0, *order]:
        for ys in [0, *near_first]:
            j = 1 if ys == 2 else 0
            if ys == 2:
                near = ("near_arrived", k, 3 if k in (0, 3) else 1)
                add("pass_far", (k,), [near, *all_x], [(("far", k), "yu" if k in (0, 3) else "yd", piece)], 0.0, 0)
                add("far_arrived", (k,), [("far", k)], [(("pair", k, 2), "d", piece)] if plan.nc > 1 else [], CUT_A, 1)
                cuts[1].append(("far_arrived", k))
            elif ys:
                add("near_arrived", (k, ys), [("near", k, ys)], [(("pair", k, ys), "d", piece)] if plan.nc > 1 else [], CUT_A, 1)
                cuts[0].append(("near_arrived", k, ys))
            if plan.nc > 1:
                add("pair_arrived", (k, ys), [("pair", k, ys)], [], CUT_A, 2)
                cuts[j].append(("pair_arrived", k, ys))
    b_cuts = {n: [] for n in chunks}
    for n in chunks:
        for g, (_, slots, _) in enumerate(groups[n]):
            if n == 0:
                far_y = [0, *near_first][g]
                keys = [("b_in", n, k, q) for k in [0, *near_first] for q in range(plan.nc) if (k or q) and (k + far_y) % plan.ny == 0]
            else:
                keys = [("b_in", n, k, q) for k in [0, *near_first] for q in range(plan.nc) if k or q] + [("ring_arrived", 0, min(HOLD[0], len(groups[0]) - 1), HOLD[1])] * (plan.nz == 8)
            keys = keys or ["go"]
            if g:
                keys.append(("b_arrived", n, g - 1))
            ups = [up for up in (True, False) if last_hop(n, g, up)]
            last = g == len(groups[n]) - 1
            sends = [(("ring", n, g, up, 1), "zu" if up else "zd", slot(n) * slots) for up in ups]
            add("b_arrived", (n, g), keys, sends, CUT_B * last, 0)
            if last:
                b_cuts[n].append(("b_arrived", n, g))
            for hop in range(1, max(last_hop(n, g, True), last_hop(n, g, False)) + 1):
                keys = [("ring", n, g, up, hop) for up in ups if hop <= last_hop(n, g, up)]
                if g:
                    keys.append(("ring_arrived", n, g - 1, hop))
                sends = [(("ring", n, g, up, hop + 1), "zu" if up else "zd", slot(n) * slots) for up in ups if hop < last_hop(n, g, up)]
                add("ring_arrived", (n, g, hop), keys, sends, CUT_B * last * (1 if 2 * hop == plan.nz else 2), 0)
                if last:
                    b_cuts[n].append(("ring_arrived", n, g, hop))
    for n in chunks:
        for j in range(2):
            slots = len(row_parts[j]) * plan.nc
            if not slots:
                continue
            half = slot(n) * slots / 2
            before = cuts[j] + b_cuts[n]
            sets = [(0,)]
            if plan.nx == 4:
                sets = GROUPS[j, n]
            for ds in sets:
                columns = 256 * (-(-2 * widths[n] // 256) + -(-widths[n] // 256))
                cost = 0.25 + DOT * len(ds) * slots * 32 * columns * inner / 1e6
                sends = []
                for d in ds:
                    if d == 2:
                        sends += [(("turn", j, n, 0), "xu", half), (("turn", j, n, 1), "xd", half)]
                    elif d:
                        sends += [(("got", j, n, d, 0), "xu" if d == 1 else "xd", half)]
                add("product", (j, n, ds), before, ["late", *sends], cost, 6 + n - 0.5 * j)
                before = [*before, ("product", j, n, ds)]
            done = before[-1]
            keys = []
            if plan.nx == 4:
                add("pass_on", (j, n), [("turn", j, n, 0), ("turn", j, n, 1), ("product", j, n, next(ds for ds in sets if 3 in ds))], ["late", (("got", j, n, 1, 1), "xu", half), (("got", j, n, 3, 1), "xd", half)], 0.2, 3)
                keys = [("got", j, n, d, i) for d in (1, 3) for i in (0, 1)] + [("pass_on", j, n)]
            sends = ["late"] + [(("back", n, k, q), {0: "d", 1: "yu", 2: ("yu", "yd")[q], 3: "yd"}[k], slot(n) * (2 if k == 2 else 1)) for k in row_parts[j] for q in range(plan.nc) if k or q]
            add("finish", (j, n), [*keys, done], sends, 0.3, 3)
        ends = [("finish", j, n) for j in range(2) if row_parts[j]]
        pieces = [(k, q) for k in [0, *near_first] for q in range(plan.nc) if k or q]
        add("hand_over", (n,), [*ends, *(("back", n, *piece) for piece in pieces)], [], 0.3, 4 + n)

    out = []
    while steps:
        able = [(max(known[d] for d in s[2]), i) for i, s in enumerate(steps) if all(d in known for d in s[2])]
        now = [(steps[i][5], when, i) for when, i in able if when <= clock[0]]
        i = min(now)[2] if now else min(able)[1]
        act, what, deps, sends, cost, _ = steps.pop(i)
        clock[0] = max(clock[0], max(known[d] for d in deps)) + 0.05
        late = bool(sends) and sends[0] == "late"
        if late:
            clock[0] += cost
        for key, link, size in sends[1:] if late else sends:
            speed = 300.0 if link == "d" else rate * 1024 / 1000 * 0.98
            begun = max(clock[0], free.get(link, 0.0))
            free[link] = begun + size / speed
            known[key] = free[link] + (0.9 if link == "d" else LAG)
        if not late:
            clock[0] += cost
        known[(act, *what)] = clock[0]
        out.append((clock[0], act, what))
    first = (("send_b", (0,)), ("x_send", ()), ("spread", (0,)))
    return [(when, act, what) for when, act, what in out if (act, what) not in first]


def exchange_product(plan, widths, a_rows, b_rows):
    nx, nz, nc, nyc = plan.nx, plan.nz, plan.nc, plan.nyc
    nb, ni, nh, na, deep = a_rows.shape
    inner = nh * na * deep // nx
    f32, bf16 = jnp.float32, jnp.bfloat16
    slots = [min(3, plan.ny) * nc, nc] if plan.ny == 4 else [nyc, nc]

    def per_part(of):
        return [[pltpu.VMEM(of(s, w), f32) for w in widths] for s in slots]

    return pl.pallas_call(
        functools.partial(kernel, plan),
        out_shape=jax.ShapeDtypeStruct(b_rows.shape, f32),
        in_specs=[pl.BlockSpec(memory_space=pl.ANY)] * 2,
        out_specs=pl.BlockSpec(memory_space=pltpu.VMEM),
        scratch_shapes=[
            pltpu.VMEM((nx, 32, inner), f32),
            pltpu.VMEM((nx, nyc, 32, inner), f32),
            [pltpu.VMEM((nx, s * 32, inner), bf16) for s in slots],
            [pltpu.VMEM((nx, s * 32, inner), bf16) for s in slots],
            [pltpu.VMEM((nyc, nb, ni, w), f32) for w in widths],
            [pltpu.VMEM((nz, nyc, nb, ni, w), f32) for w in widths],
            [pltpu.VMEM((inner, 2 * w), bf16) for w in widths],
            per_part(lambda s, w: (nx, s, 32, w)),
            per_part(lambda s, w: (1, s, 32, w)),
            per_part(lambda s, w: (2, s, 32, w)),
            per_part(lambda s, w: (s, 32, w)),
            [pltpu.VMEM((nyc, 32, w), f32) for w in widths],
            pltpu.VMEM(a_rows.shape, f32),
            pltpu.VMEM(b_rows.shape, f32),
            pltpu.SemaphoreType.DMA((2,)),
            pltpu.SemaphoreType.DMA((150,)),
            pltpu.SemaphoreType.DMA((150,)),
        ],
        compiler_params=pltpu.CompilerParams(
            collective_id=0, has_side_effects=True, vmem_limit_bytes=60 * 1024 * 1024
        ),
    )(a_rows, b_rows)


def solution(mesh):
    plan = Plan(4, 4, mesh.shape["str"] // 4, 2)
    spec = P(None, ("cls", "str"), None, None, None)
    return jax.shard_map(
        functools.partial(exchange_product, plan, WIDTHS),
        mesh=mesh,
        in_specs=(spec, spec),
        out_specs=spec,
        check_vma=False,
    )
```

time: 98.3 us -> 78.8 us (0.80)
  Pallas kernels: 90.7 us -> 76.7 us
  local copies, waits for them, and re-layouts: 7.33 us -> 1.87 us
    pallas_call x1, Pallas kernels: 90.7 us -> 76.7 us  [exchange_product(): pl.pallas_call(functools.partial(kernel, plan), out_shape=jax.ShapeDtypeS...]
    reshape x5 -> x0, local copies, waits for them, and re-layouts: 5.79 us -> none  [the longest x2 2.15 us: local(): a_parts = first_factor_tiles.reshape(b * i, h * c, plan.nx, r // plan.nx)]
where the time goes in v2:
time: 78.8 us; the launch traced here: 78.6 us
  Pallas kernels  76.7 us (97%)
  local copies, waits for them, and re-layouts  1.87 us (2%)
    pallas_call x1, Pallas kernels, exchange_product(): pl.pallas_call(functools.partial(kernel, plan), out_shape=jax.ShapeDtypeS...  76.7 us
    unnamed x1, local copies, waits for them, and re-layouts  1.87 us

profile of v2, /device:TPU:1, one launch (start us, length us, event | category | flops | bytes accessed | tf_op | source)
XLA Modules:
  0.0 78.6 jit_solution(2095670600881129703)
XLA Ops:
  0.0 76.7 %shard_map.28 = f32[8,4,2,4,512]{4,3,2,1,0:T(4,128)} custom-call(f32[8,4,2,4,1024]{4,3,2,1,0:T(4,128)} %a_hbm.1, f32[8,4,2,4,512]{4,3,2,1,0:T(4,128)} %b_hbm.1), custom_call_target="tpu_custom_call" | custom-call | tf_op jit(solution)/shard_map/pallas_call | solution.py:465
  76.8 1.9 %copy.4 = f32[8,4,2,4,512]{4,3,2,1,0:T(4,128)} copy(f32[8,4,2,4,512]{4,3,2,1,0:T(4,128)} %shard_map.28) | data formatting | bytes 1048576

commit v3 on v2

--- a/solution.py
+++ b/solution.py
@@ -8,15 +8,17 @@
 from jax.sharding import PartitionSpec as P
 
 MESH = pl.DeviceIdType.MESH
-WIDTHS = (384, 128)
+WIDTHS = (256, 128, 128)
 LAG, CUT_A, CUT_B, DOT = 2.8, 0.2, 0.25, 0.0022
 GROUPS = {
-    (0, 0): ((2,), (1,), (3,), (0,)),
+    (0, 0): ((2, 1), (3, 0)),
     (0, 1): ((2, 1), (3, 0)),
+    (0, 2): ((2, 1), (3, 0)),
     (1, 0): ((2, 1, 3, 0),),
     (1, 1): ((2, 1, 3, 0),),
+    (1, 2): ((2, 1, 3, 0),),
 }
-HOLD = (3, 2)
+HOLD = {1: (0, 1, 3), 2: (0, 4, 3)}
 
 
 class Plan:
@@ -182,28 +184,27 @@
 
         lax.fori_loop(0, nb, one, 0)
 
-    groups = {0: [(ymod(k) * nc, nc, k in (0, 1)) for k in [0, *near_first]]}
-    wide = max(1, nyc // 2) if ny > 1 else nyc
-    for n in chunks[1:]:
-        groups[n] = [(first, wide, first == 0) for first in range(0, nyc, wide)]
+    groups = {}
+    for n in chunks:
+        groups[n] = [(yc, 1, True, [])]
+        if nc > 1:
+            groups[n].append((y * nc + cmod(1), 1, True, [(0, 1)]))
+        for k in near_first:
+            keys = [((ny - k) % ny, q) for q in range(nc)]
+            groups[n].append((ymod(k) * nc, nc, k == 1, keys))
+
     rings = {}
 
     def last_hop(n, g, up):
         return nz // 2 if groups[n][g][2] == up else (nz - 1) // 2
 
     def ring(n, g, up, hop):
-        first, slots, _ = groups[n][g]
+        first, slots = groups[n][g][:2]
         there = bt[n].at[zmod(1 - hop if up else hop - 1), pl.ds(first, slots)]
         rings[n, g, up, hop] = push(there, there, z_next if up else z_prev)
 
     def b_arrived(n, g):
-        keys = list(others)
-        if n == 0:
-            far_y = [0, *near_first][g]
-            keys = [(k, q) for k, q in others if (k + far_y) % ny == 0]
-        elif g:
-            keys = []
-        for k, q in keys:
+        for k, q in groups[n][g][3]:
             b_in[n, k, q].wait_recv()
         for up in (True, False):
             if last_hop(n, g, up):
@@ -374,13 +375,10 @@
                 cuts[j].append(("pair_arrived", k, ys))
     b_cuts = {n: [] for n in chunks}
     for n in chunks:
-        for g, (_, slots, _) in enumerate(groups[n]):
-            if n == 0:
-                far_y = [0, *near_first][g]
-                keys = [("b_in", n, k, q) for k in [0, *near_first] for q in range(plan.nc) if (k or q) and (k + far_y) % plan.ny == 0]
-            else:
-                keys = [("b_in", n, k, q) for k in [0, *near_first] for q in range(plan.nc) if k or q] + [("ring_arrived", 0, min(HOLD[0], len(groups[0]) - 1), HOLD[1])] * (plan.nz == 8)
-            keys = keys or ["go"]
+        for g, (_, slots, _, pieces) in enumerate(groups[n]):
+            keys = [("send_b", n), *(("b_in", n, *piece) for piece in pieces)]
+            if n and plan.nz == 8 and plan.ny == 4:
+                keys.append(("ring_arrived", *HOLD[n]))
             if g:
                 keys.append(("b_arrived", n, g - 1))
             ups = [up for up in (True, False) if last_hop(n, g, up)]
@@ -464,7 +462,7 @@
 
     return pl.pallas_call(
         functools.partial(kernel, plan),
-        out_shape=jax.ShapeDtypeStruct(b_rows.shape, f32),
+        out_shape=pltpu.VMEM(b_rows.shape, f32),
         in_specs=[pl.BlockSpec(memory_space=pl.ANY)] * 2,
         out_specs=pl.BlockSpec(memory_space=pltpu.VMEM),
         scratch_shapes=[
@@ -483,8 +481,8 @@
             pltpu.VMEM(a_rows.shape, f32),
             pltpu.VMEM(b_rows.shape, f32),
             pltpu.SemaphoreType.DMA((2,)),
-            pltpu.SemaphoreType.DMA((150,)),
-            pltpu.SemaphoreType.DMA((150,)),
+            pltpu.SemaphoreType.DMA((240,)),
+            pltpu.SemaphoreType.DMA((240,)),
         ],
         compiler_params=pltpu.CompilerParams(
             collective_id=0, has_side_effects=True, vmem_limit_bytes=60 * 1024 * 1024

time: 78.8 us -> 76.7 us (0.973)
  local copies, waits for them, and re-layouts: 1.87 us -> 0.8 us
  Pallas kernels: 76.7 us -> 75.8 us
    unnamed x1, local copies, waits for them, and re-layouts: 1.87 us -> 0.8 us
    pallas_call x1, Pallas kernels: 76.7 us -> 75.8 us  [exchange_product(): pl.pallas_call(functools.partial(kernel, plan), out_shape=pltpu.VMEM(b_ro...]
where the time goes in v3:
time: 76.7 us; the launch traced here: 76.6 us
  Pallas kernels  75.8 us (99%)
  local copies, waits for them, and re-layouts  0.8 us (1%)
    pallas_call x1, Pallas kernels, exchange_product(): pl.pallas_call(functools.partial(kernel, plan), out_shape=pltpu.VMEM(b_ro...  75.8 us

profile of v3, /device:TPU:1, one launch (start us, length us, event | category | flops | bytes accessed | tf_op | source)
XLA Modules:
  0.0 76.6 jit_solution(3540899382284353549)
XLA Ops:
  0.0 75.8 %shard_map.28 = f32[8,4,2,4,512]{4,3,2,1,0:T(4,128)S(1)} custom-call(f32[8,4,2,4,1024]{4,3,2,1,0:T(4,128)} %a_hbm.1, f32[8,4,2,4,512]{4,3,2,1,0:T(4,128)} %b_hbm.1), custom_call_target="tpu_custom_call" | custom-call | tf_op jit(solution)/shard_map/pallas_call | solution.py:463
  75.8 0.8 %copy.4 = f32[8,4,2,4,512]{4,3,2,1,0:T(4,128)} copy(f32[8,4,2,4,512]{4,3,2,1,0:T(4,128)S(1)} %shard_map.28) | data formatting | bytes 1048576

commit v4 on v3

--- a/solution.py
+++ b/solution.py
@@ -324,10 +324,11 @@
     cut_a(0, 0, True)
     inner = asrc.shape[2]
     plans = schedule(plan, order, near_first, groups, last_hop, row_parts, chunks, widths, inner)
-    for _, act, what in plans:
+    for _, act, what in plans[:-1]:
         acts[act](*what)
     for copy in started:
         copy.wait_send()
+    acts[plans[-1][1]](*plans[-1][2])
 
 
 def schedule(plan, order, near_first, groups, last_hop, row_parts, chunks, widths, inner):

time: 76.7 us -> 76.4 us (level)
  no operation moved by 1% of the time
where the time goes in v4:
time: 76.4 us; the launch traced here: 76.3 us
  Pallas kernels  75.5 us (99%)
  local copies, waits for them, and re-layouts  0.8 us (1%)
    pallas_call x1, Pallas kernels, exchange_product(): pl.pallas_call(functools.partial(kernel, plan), out_shape=pltpu.VMEM(b_ro...  75.5 us

profile of v4, /device:TPU:1, one launch (start us, length us, event | category | flops | bytes accessed | tf_op | source)
XLA Modules:
  0.0 76.3 jit_solution(4906825838717541924)
XLA Ops:
  0.0 75.5 %shard_map.28 = f32[8,4,2,4,512]{4,3,2,1,0:T(4,128)S(1)} custom-call(f32[8,4,2,4,1024]{4,3,2,1,0:T(4,128)} %a_hbm.1, f32[8,4,2,4,512]{4,3,2,1,0:T(4,128)} %b_hbm.1), custom_call_target="tpu_custom_call" | custom-call | tf_op jit(solution)/shard_map/pallas_call | solution.py:464
  75.5 0.8 %copy.4 = f32[8,4,2,4,512]{4,3,2,1,0:T(4,128)} copy(f32[8,4,2,4,512]{4,3,2,1,0:T(4,128)S(1)} %shard_map.28) | data formatting | bytes 1048576
